TPU v7x, 128 devices: a whole 4x4x4 slice. The times are simulated.
128 devices in a mesh: tm: 32 (over y, x, core), grp: 4 (over z).
Axes of the slice: x: 4, y: 4, z: 4, core: 2. Of those that a mesh axis runs over, the one named last changes fastest.
Arguments:
- series: float32 [524288, 512], P(('tm', 'grp')), may hold values from -6 to 6
- filter_taps: float32 [33], replicated, may hold values from -1 to 1
- sign_flips: int32 [524288], P(('tm', 'grp')), may hold values from -1 to 1, as said below
- samples: int32 [8192], replicated, may hold values from 0 to 524287, as said below
Outputs:
- sketch: float32 [8192, 512], P(('tm', 'grp'))
- r_factor: float32 [512, 512], replicated
Inputs may be any that keep to these rules, and one draw needn't show every extreme that they name: `sign_flips`: each entry is -1 or +1. All distinct; the values of samples modulo 4096 take exactly 4096 distinct values, each by exactly 2 consecutive entries; entries are ordered by their value modulo 4096, then by value.
All inputs are finite; a program needn't handle non-finite values.
Results may differ from a plain program's by a relative error of at most 0.0003.
Values sent between devices are 32-bit elements; how exact they have to be, the bound alone decides.
No kernel may reach another device: no remote copies, remote signals or barrier semaphores. Data moves between devices by JAX's collectives and lax.ppermute only.
A program may use at most 128 MiB of HBM per device.

v0:
```python
import jax
import jax.numpy as jnp
from jax import lax
from jax.sharding import PartitionSpec as P


def with_halo(array, sides, width):
    edges = {}
    for axis, dim in sides:
        size, length = (lax.axis_size(axis), array.shape[dim])
        up = [(i, (i + 1) % size) for i in range(size - 1)]
        last = lax.slice_in_dim(array, length - width, length, axis=dim)
        leading = lax.slice_in_dim(array, 0, width, axis=dim)
        edges[dim] = (
            lax.ppermute(last, axis, up),
            lax.ppermute(leading, axis, [(b, a) for a, b in up]),
        )
    done = []
    for _, dim in sides:
        low, high = edges[dim]
        around = [(width, width) if d in done else (0, 0) for d in range(array.ndim)]
        array = jnp.concatenate([jnp.pad(low, around), array, jnp.pad(high, around)], axis=dim)
        done.append(dim)
    return array


def bit_count(values, width_bits):
    counted = jnp.zeros_like(values)
    for offset in range(width_bits):
        counted = counted + (values >> offset & 1)
    return counted


def hadamard(order):
    row_ids = jnp.arange(order, dtype=jnp.int32)[:, None]
    col_ids = jnp.arange(order, dtype=jnp.int32)[None, :]
    parity = bit_count(row_ids & col_ids, max(order.bit_length(), 1)) & 1
    return (1 - 2 * parity).astype(jnp.float32)


def local_transform(rows_block):
    length, columns = rows_block.shape
    levels = length.bit_length() - 1
    outer = 2 ** ((levels + 1) // 2)
    inner = length // outer
    layered = rows_block.reshape(outer, inner, columns)
    layered = jnp.einsum("ux,xvw->uvw", hadamard(outer), layered, precision=lax.Precision.HIGHEST)
    layered = jnp.einsum("vy,uyw->uvw", hadamard(inner), layered, precision=lax.Precision.HIGHEST)
    return layered.reshape(length, columns)


def on_device(series, filter_taps, sign_flips, samples):
    rows_dev = series.shape[0]
    columns = series.shape[1]
    tap_count = filter_taps.shape[0]
    half_taps = (tap_count - 1) // 2
    devices_all = lax.axis_size("tm") * lax.axis_size("grp")
    total_rows = rows_dev * devices_all
    sample_count = samples.shape[0]
    padded = with_halo(series, ((("tm", "grp"), 0),), half_taps)
    filtered = filter_taps[0] * padded[0:rows_dev]
    for offset in range(1, tap_count):
        filtered = filtered + filter_taps[offset] * padded[offset : offset + rows_dev]
    flipped = filtered * sign_flips.astype(jnp.float32)[:, None]
    mixed = local_transform(flipped)
    position = lax.axis_index("tm") * lax.axis_size("grp") + lax.axis_index("grp")
    row_scale = 1.0 / jnp.sqrt(jnp.float32(total_rows))
    block_rows = sample_count // devices_all
    copies = max(2, sample_count // rows_dev)
    distinct = sample_count // copies
    per_device = distinct // devices_all
    used_positions = samples[::copies] % rows_dev
    outgoing = jnp.take(mixed, used_positions, axis=0)
    incoming = lax.all_to_all(outgoing, ("tm", "grp"), split_axis=0, concat_axis=0, tiled=True)
    stacked = incoming.reshape(devices_all, per_device, columns)
    combined = (
        jnp.einsum("op,pkw->okw", hadamard(devices_all), stacked, precision=lax.Precision.HIGHEST)
        * row_scale
    )
    combined = combined.reshape(devices_all * per_device, columns)
    mine = lax.dynamic_slice_in_dim(samples, position * block_rows, block_rows)
    slot_index = mine // rows_dev * per_device + jnp.arange(block_rows, dtype=jnp.int32) // copies
    sketch = jnp.take(combined, slot_index, axis=0)
    local_gram = lax.dot_general(
        sketch,
        sketch,
        (((0,), (0,)), ((), ())),
        precision=lax.Precision.HIGHEST,
        preferred_element_type=jnp.float32,
    )
    gram = lax.psum(local_gram, ("tm", "grp"))
    lower = jnp.linalg.cholesky(gram / sample_count)
    return (sketch, lower.T)


def solution(mesh):
    return jax.shard_map(
        on_device,
        mesh=mesh,
        in_specs=(P(("tm", "grp"), None), P(), P(("tm", "grp")), P()),
        out_specs=(P(("tm", "grp"), None), P()),
        check_vma=False,
    )
```

profile of v0, /device:TPU:1, one launch (start us, length us, event | category | flops | bytes accessed | tf_op | source)
XLA Modules:
  0.0 597.2 jit_solution(11944672422323260254)
XLA Ops:
  7.2 0.8 fusion.120
  7.9 4.4 collective-permute-start
  12.3 4.6 collective-permute-start.1
  16.9 1.4 slice.317
  18.3 2.1 fusion.121
  20.4 1.9 fusion.122
  22.3 0.7 convert_element_type.14
  23.0 0.1 broadcast_in_dim.36
  23.1 0.6 constant_dynamic-update-slice_fusion.1
  23.7 11.5 %constant_dynamic-update-slice_fusion = (f32[4112,512]{1,0:T(8,128)}, f32[4112,512]{1,0:T(8,128)}) fusion(f32[4112,512]{1,0:T(8,128)} %constant_dynamic-update-slice_fusion.1, f32[4096,512]{1,0:T(8,128)} %param.4), kind=kLoop, calls=%fused_computation.157 | loop fusion | bytes 25165824 | tf_op jit(solution)/shard_map/concatenate | solution.py:22
  35.3 0.6 constant_dynamic-update-slice_fusion.2
  35.9 122.7 %fusion.1 = f32[4096,512]{1,0:T(8,128)S(1)} fusion(f32[4112,512]{1,0:T(8,128)} %constant_dynamic-update-slice_fusion.2, f32[4112,512]{1,0:T(8,128)} %get-tuple-element.10, f32[4096,512]{1,0:T(8,128)} %param.4, f32[4096]{0:T(1024)S(1)} %convert_element_type.14, f32[]{:T(128)} %bitcast.34, f32[]{:T(128)} %bitcast.33, f32[]{:T(128)} %bitcast.32, f32[]{:T(128)} %bitcast.31, ...), kind=kLoop, calls=%fused_computation.4 | loop fusion | flops 138412032 | bytes 285229184 | tf_op jit(solution)/shard_map/mul | solution.py:64
  158.6 12.4 %fusion.37 = f32[64,64,512]{2,0,1:T(8,128)S(1)} fusion(f32[64,64,512]{2,1,0:T(8,128)S(1)} %bitcast.75), kind=kOutput, calls=%fused_computation.71 | convolution fusion | flops 1610715136 | bytes 16777216 | tf_op jit(solution)/shard_map/ux,xvw->uvw/dot_general | solution.py:47
  171.0 13.7 %fusion.35 = f32[64,512,64]{1,2,0:T(8,128)} fusion(f32[64,64,512]{2,0,1:T(8,128)S(1)} %fusion.37), kind=kOutput, calls=%fused_computation.69 | convolution fusion | flops 1610715136 | bytes 16777216 | tf_op jit(solution)/shard_map/vy,uyw->uvw/dot_general | solution.py:48
  184.8 21.4 %gather_fusion = f32[4096,512]{1,0:T(8,128)} fusion(f32[4096,512]{1,0:T(8,128)} %bitcast.73, s32[4096]{0:T(1024)S(1)} %broadcast_clamp_fusion), kind=kCustom, calls=%fused_computation | custom fusion | bytes 16793600 | tf_op jit(solution)/shard_map/jit(_take)/gather | solution.py:73
  206.2 5.8 broadcast_select_fusion
  212.0 8.8 %all-to-all-start = ((f32[128,32,512]{2,1,0:T(8,128)}), f32[128,32,512]{2,1,0:T(8,128)}, u32[]{:S(2)}, u32[]{:S(2)}) async-start(f32[128,32,512]{2,1,0:T(8,128)} %broadcast_select_fusion), calls=%async_computation | async-start | bytes 16777216 | tf_op jit(solution)/shard_map/all_to_all | solution.py:74
  220.8 0.0 all-reduce.3.cloned.1.call-start
  220.9 0.8 compare_and_fusion.1
  221.7 101.7 %all-to-all-done = f32[128,32,512]{2,1,0:T(8,128)} async-done(((f32[128,32,512]{2,1,0:T(8,128)}), f32[128,32,512]{2,1,0:T(8,128)}, u32[]{:S(2)}, u32[]{:S(2)}) %all-to-all-start) | async-done | bytes 8388640 | tf_op jit(solution)/shard_map/all_to_all | solution.py:74
  323.4 17.0 %broadcast_multiply_fusion = f32[128,32,512]{2,0,1:T(8,128)S(1)} fusion(f32[128,32,512]{2,1,0:T(8,128)} %all-to-all-done), kind=kOutput, calls=%fused_computation.73 | convolution fusion | flops 3223781376 | bytes 16777216 | tf_op jit(solution)/shard_map/op,pkw->okw/dot_general | solution.py:77
  340.5 8.1 %copy.18 = f32[128,32,512]{2,1,0:T(8,128)} copy(f32[128,32,512]{2,0,1:T(8,128)S(1)} %broadcast_multiply_fusion) | data formatting | bytes 16777216 | tf_op jit(solution)/shard_map/mul | solution.py:77
  348.5 4.1 gather_fusion.1
  352.6 0.1 broadcast_select_fusion.1
  352.7 2.0 fusion.123
  354.8 147.3 %all-reduce.3.cloned.1.call-done = f32[512,512]{0,1:T(8,128)} async-done(((f32[512,512]{0,1:T(8,128)}), f32[512,512]{0,1:T(8,128)}) %all-reduce.3.cloned.1.call-update) | async-done | bytes 1048592 | tf_op jit(solution)/shard_map/psum | solution.py:91
  502.0 1.3 broadcast_multiply_fusion.1
  503.4 0.3 copy.20
  503.7 1.5 fusion.41
  505.2 11.7 %cholesky.104 = f32[128,128]{1,0:T(8,128)S(1)} custom-call(f32[128,128]{1,0:T(8,128)S(1)} %cholesky.266), custom_call_target="Cholesky" | custom-call | tf_op jit(solution)/shard_map/jit(cholesky)/cholesky | solution.py:92
  516.9 0.1 cholesky.224
  517.1 10.0 %custom-call.27 = f32[1,128,128]{1,2,0:T(8,128)S(1)} custom-call(f32[1,128,128]{2,1,0:T(8,128)S(1)} %get-tuple-element.23), custom_call_target="InvertDiagBlocksLowerTriangular" | custom-call | tf_op jit(solution)/shard_map/jit(cholesky)/cholesky | solution.py:92
  527.1 0.3 constant_dynamic-update-slice_fusion.6
  527.4 0.3 convolution_subtract_fusion
  527.8 11.7 %cholesky.217 = f32[128,128]{1,0:T(8,128)S(1)} custom-call(f32[128,128]{1,0:T(8,128)S(1)} %cholesky.270), custom_call_target="Cholesky" | custom-call | tf_op jit(solution)/shard_map/jit(cholesky)/cholesky | solution.py:92
  539.5 9.8 %custom-call.28 = f32[1,128,128]{1,2,0:T(8,128)S(1)} custom-call(f32[1,128,128]{2,1,0:T(8,128)S(1)} %get-tuple-element.20), custom_call_target="InvertDiagBlocksLowerTriangular" | custom-call | tf_op jit(solution)/shard_map/jit(cholesky)/cholesky | solution.py:92
  549.3 0.3 convolution_dynamic-update-slice_fusion
  549.6 0.4 convolution_subtract_fusion.1
  550.0 11.7 %cholesky.238 = f32[128,128]{1,0:T(8,128)S(1)} custom-call(f32[128,128]{1,0:T(8,128)S(1)} %cholesky.275), custom_call_target="Cholesky" | custom-call | tf_op jit(solution)/shard_map/jit(cholesky)/cholesky | solution.py:92
  561.7 10.0 %custom-call.29 = f32[1,128,128]{1,2,0:T(8,128)S(1)} custom-call(f32[1,128,128]{2,1,0:T(8,128)S(1)} %get-tuple-element.17), custom_call_target="InvertDiagBlocksLowerTriangular" | custom-call | tf_op jit(solution)/shard_map/jit(cholesky)/cholesky | solution.py:92
  571.8 0.2 convolution_dynamic-update-slice_fusion.1
  572.0 0.4 convolution_subtract_fusion.2
  572.4 11.7 %cholesky.255 = f32[128,128]{1,0:T(8,128)S(1)} custom-call(f32[128,128]{1,0:T(8,128)S(1)} %convolution_subtract_fusion.2), custom_call_target="Cholesky" | custom-call | tf_op jit(solution)/shard_map/jit(cholesky)/cholesky | solution.py:92
  584.1 0.7 compare_reduce_fusion.1
  584.9 0.6 compare_reduce_fusion
  585.5 0.7 compare_reduce_fusion.2
  588.7 0.1 select_bitcast_fusion
  588.8 1.3 copy.21
  (15 shorter events, 0.2 us)
Async XLA Ops:
  7.9 15.2 %collective-permute-start = (f32[16,512]{1,0:T(8,128)S(1)}, f32[16,512]{1,0:T(8,128)S(1)}, u32[]{:S(2)}, u32[]{:S(2)}) collective-permute-start(f32[16,512]{1,0:T(8,128)S(1)} %get-tuple-element.12), channel_id=1, source_target_pairs={{0,1},{1,2},{2,3},{3,4},{4,5},{5,6},{6,7},{7,8},{8,9},{9,10},{10,1... | collective-permute-start | bytes 98312 | tf_op jit(solution)/shard_map/ppermute | solution.py:15
  12.3 23.0 %collective-permute-start.1 = (f32[16,512]{1,0:T(8,128)S(1)}, f32[16,512]{1,0:T(8,128)S(1)}, u32[]{:S(2)}, u32[]{:S(2)}) collective-permute-start(f32[16,512]{1,0:T(8,128)S(1)} %get-tuple-element.13), channel_id=1, source_target_pairs={{1,0},{2,1},{3,2},{4,3},{5,4},{6,5},{7,6},{8,7},{9,8},{10,9},{11,1... | collective-permute-start | bytes 98312 | tf_op jit(solution)/shard_map/ppermute | solution.py:16
  212.0 111.4 %all-to-all-start = ((f32[128,32,512]{2,1,0:T(8,128)}), f32[128,32,512]{2,1,0:T(8,128)}, u32[]{:S(2)}, u32[]{:S(2)}) async-start(f32[128,32,512]{2,1,0:T(8,128)} %broadcast_select_fusion), calls=%async_computation | async-start | bytes 16777216 | tf_op jit(solution)/shard_map/all_to_all | solution.py:74
  220.8 281.2 %all-reduce.3.cloned.1.call-start = ((), (), s32[]{:S(2)}) async-start(), calls=%async_computation.1 | async-start | bytes 2097152 | tf_op jit(solution)/shard_map/psum | solution.py:91
  352.7 236.1 %copy-start = (f32[64,512]{1,0:T(8,128)}, f32[64,512]{1,0:T(8,128)S(1)}, u32[]{:S(2)}) copy-start(f32[64,512]{1,0:T(8,128)S(1)} %broadcast_select_fusion.1) | copy-start | bytes 393220
Sparse Core Ops, SparseCore 0:
  354.9 147.1 all-reduce.2
where the time goes:
time: 602 us; the launch traced here: 597 us
  waiting for transfers between devices  249 us (41%)
  other arithmetic  212 us (35%)
  local copies, waits for them, and re-layouts  54.3 us (9%)
  matrix products  47.1 us (8%)
  starting transfers between devices  17.8 us (3%)
  between operations  17.1 us (3%)
    psum x1, waiting for transfers between devices, on_device(): gram = lax.psum(local_gram, ('tm', 'grp'))  147 us
    mul x1, other arithmetic, on_device(): flipped = filtered * sign_flips.astype(jnp.float32)[:, None]  123 us
    all_to_all x1, waiting for transfers between devices, on_device(): lax.all_to_all(outgoing, ('tm', 'grp'), split_axis=0, concat_axis=0, tile...  102 us
    another operation x14, other arithmetic, on_device(): lower = jnp.linalg.cholesky(gram / sample_count)  78.9 us
    gather x1, local copies, waits for them, and re-layouts, on_device(): outgoing = jnp.take(mixed, used_positions, axis=0)  21.4 us
    dot_general x1, matrix products, on_device(): jnp.einsum('op,pkw->okw', hadamard(devices_all), stacked, precision=lax.P...  17 us
    dot_general x1, matrix products, local_transform(): jnp.einsum('vy,uyw->uvw', hadamard(inner), layered, precision=lax.Precisi...  13.7 us
    dot_general x1, matrix products, local_transform(): jnp.einsum('ux,xvw->uvw', hadamard(outer), layered, precision=lax.Precisi...  12.4 us
  transfers between devices with their start and end apart: 4, of which 2 were waited for; matrix products, arithmetic and copies ran while one was open for 3% of the time, Pallas kernels for 0%

commit v1 on v0

--- a/solution.py
+++ b/solution.py
@@ -88,7 +88,9 @@
         precision=lax.Precision.HIGHEST,
         preferred_element_type=jnp.float32,
     )
-    gram = lax.psum(local_gram, ("tm", "grp"))
+    gram = local_gram
+    for mesh_axis in ("grp", "tm"):
+        gram = lax.psum(gram, mesh_axis)
     lower = jnp.linalg.cholesky(gram / sample_count)
     return (sketch, lower.T)
 

time: 602 us -> 609 us (1.012)
  waiting for transfers between devices: 249 us -> 256 us
    psum x1 -> x2, waiting for transfers between devices: 147 us -> 154 us  [on_device(): gram = lax.psum(gram, mesh_axis)]
  transfers between devices with their start and end apart: 4 -> 5, of which waited for: 2 -> 3; matrix products, arithmetic and copies ran while one was open for 3% -> 3% of each run, Pallas kernels for 0% -> 0%
where the time goes in v1:
time: 609 us; the launch traced here: 604 us
  waiting for transfers between devices  256 us (42%)
  other arithmetic  212 us (35%)
  local copies, waits for them, and re-layouts  54.3 us (9%)
  matrix products  47.4 us (8%)
  starting transfers between devices  18 us (3%)
  between operations  17.1 us (3%)
    psum x2, waiting for transfers between devices, on_device(): gram = lax.psum(gram, mesh_axis)  154 us
    mul x1, other arithmetic, on_device(): flipped = filtered * sign_flips.astype(jnp.float32)[:, None]  123 us
    all_to_all x1, waiting for transfers between devices, on_device(): lax.all_to_all(outgoing, ('tm', 'grp'), split_axis=0, concat_axis=0, tile...  102 us
    another operation x14, other arithmetic, on_device(): lower = jnp.linalg.cholesky(gram / sample_count)  78.6 us
    gather x1, local copies, waits for them, and re-layouts, on_device(): outgoing = jnp.take(mixed, used_positions, axis=0)  21.4 us
    dot_general x1, matrix products, on_device(): jnp.einsum('op,pkw->okw', hadamard(devices_all), stacked, precision=lax.P...  17.6 us
    dot_general x1, matrix products, local_transform(): jnp.einsum('vy,uyw->uvw', hadamard(inner), layered, precision=lax.Precisi...  13.5 us
    dot_general x1, matrix products, local_transform(): jnp.einsum('ux,xvw->uvw', hadamard(outer), layered, precision=lax.Precisi...  12.4 us
  transfers between devices with their start and end apart: 5, of which 3 were waited for; matrix products, arithmetic and copies ran while one was open for 3% of the time, Pallas kernels for 0%

profile of v1, /device:TPU:1, one launch (start us, length us, event | category | flops | bytes accessed | tf_op | source)
XLA Modules:
  0.0 604.3 jit_solution(6176581096467166493)
XLA Ops:
  7.2 0.8 fusion.120
  7.9 4.4 collective-permute-start
  12.3 4.6 collective-permute-start.1
  16.9 1.4 slice.317
  18.3 2.1 fusion.121
  20.4 1.9 fusion.122
  22.3 0.7 convert_element_type.14
  23.0 0.1 broadcast_in_dim.36
  23.1 0.6 constant_dynamic-update-slice_fusion.1
  23.7 11.5 %constant_dynamic-update-slice_fusion = (f32[4112,512]{1,0:T(8,128)}, f32[4112,512]{1,0:T(8,128)}) fusion(f32[4112,512]{1,0:T(8,128)} %constant_dynamic-update-slice_fusion.1, f32[4096,512]{1,0:T(8,128)} %param.4), kind=kLoop, calls=%fused_computation.157 | loop fusion | bytes 25165824 | tf_op jit(solution)/shard_map/concatenate | solution.py:22
  35.3 0.6 constant_dynamic-update-slice_fusion.2
  35.9 122.7 %fusion.1 = f32[4096,512]{1,0:T(8,128)S(1)} fusion(f32[4112,512]{1,0:T(8,128)} %constant_dynamic-update-slice_fusion.2, f32[4112,512]{1,0:T(8,128)} %get-tuple-element.10, f32[4096,512]{1,0:T(8,128)} %param.4, f32[4096]{0:T(1024)S(1)} %convert_element_type.14, f32[]{:T(128)} %bitcast.34, f32[]{:T(128)} %bitcast.33, f32[]{:T(128)} %bitcast.32, f32[]{:T(128)} %bitcast.31, ...), kind=kLoop, calls=%fused_computation.4 | loop fusion | flops 138412032 | bytes 285229184 | tf_op jit(solution)/shard_map/mul | solution.py:64
  158.6 12.4 %fusion.37 = f32[64,64,512]{2,0,1:T(8,128)S(1)} fusion(f32[64,64,512]{2,1,0:T(8,128)S(1)} %bitcast.75), kind=kOutput, calls=%fused_computation.71 | convolution fusion | flops 1610715136 | bytes 16777216 | tf_op jit(solution)/shard_map/ux,xvw->uvw/dot_general | solution.py:47
  171.0 13.5 %fusion.35 = f32[64,512,64]{1,2,0:T(8,128)} fusion(f32[64,64,512]{2,0,1:T(8,128)S(1)} %fusion.37), kind=kOutput, calls=%fused_computation.69 | convolution fusion | flops 1610715136 | bytes 16777216 | tf_op jit(solution)/shard_map/vy,uyw->uvw/dot_general | solution.py:48
  184.6 21.4 %gather_fusion = f32[4096,512]{1,0:T(8,128)} fusion(f32[4096,512]{1,0:T(8,128)} %bitcast.73, s32[4096]{0:T(1024)S(1)} %broadcast_clamp_fusion), kind=kCustom, calls=%fused_computation | custom fusion | bytes 16793600 | tf_op jit(solution)/shard_map/jit(_take)/gather | solution.py:73
  206.0 5.8 broadcast_select_fusion
  211.8 8.8 %all-to-all-start = ((f32[128,32,512]{2,1,0:T(8,128)}), f32[128,32,512]{2,1,0:T(8,128)}, u32[]{:S(2)}, u32[]{:S(2)}) async-start(f32[128,32,512]{2,1,0:T(8,128)} %broadcast_select_fusion), calls=%async_computation | async-start | bytes 16777216 | tf_op jit(solution)/shard_map/all_to_all | solution.py:74
  220.7 0.8 compare_and_fusion.1
  221.5 101.7 %all-to-all-done = f32[128,32,512]{2,1,0:T(8,128)} async-done(((f32[128,32,512]{2,1,0:T(8,128)}), f32[128,32,512]{2,1,0:T(8,128)}, u32[]{:S(2)}, u32[]{:S(2)}) %all-to-all-start) | async-done | bytes 8388640 | tf_op jit(solution)/shard_map/all_to_all | solution.py:74
  323.2 17.6 %broadcast_multiply_fusion = f32[128,32,512]{2,0,1:T(8,128)S(1)} fusion(f32[128,32,512]{2,1,0:T(8,128)} %all-to-all-done), kind=kOutput, calls=%fused_computation.73 | convolution fusion | flops 3223781376 | bytes 16777216 | tf_op jit(solution)/shard_map/op,pkw->okw/dot_general | solution.py:77
  340.8 8.1 %copy.18 = f32[128,32,512]{2,1,0:T(8,128)} copy(f32[128,32,512]{2,0,1:T(8,128)S(1)} %broadcast_multiply_fusion) | data formatting | bytes 16777216 | tf_op jit(solution)/shard_map/mul | solution.py:77
  348.9 4.1 gather_fusion.1
  353.1 2.0 fusion.123
  355.1 0.2 all-reduce.6.cloned.1.call-start
  355.3 43.2 %all-reduce.4.cloned.1.call-done = f32[512,512]{0,1:T(8,128)} async-done(((f32[512,512]{0,1:T(8,128)}), f32[512,512]{0,1:T(8,128)}) %all-reduce.4.cloned.1.call-update) | async-done | bytes 1048592 | tf_op jit(solution)/shard_map/psum | solution.py:93
  398.5 110.9 %all-reduce.6.cloned.1.call-done = f32[512,512]{0,1:T(8,128)} async-done(((f32[512,512]{0,1:T(8,128)}), f32[512,512]{0,1:T(8,128)}) %all-reduce.6.cloned.1.call-update) | async-done | bytes 1048592 | tf_op jit(solution)/shard_map/psum | solution.py:93
  509.4 1.3 broadcast_multiply_fusion.1
  510.7 0.3 copy.20
  511.0 1.5 fusion.41
  512.5 11.7 %cholesky.104 = f32[128,128]{1,0:T(8,128)S(1)} custom-call(f32[128,128]{1,0:T(8,128)S(1)} %cholesky.266), custom_call_target="Cholesky" | custom-call | tf_op jit(solution)/shard_map/jit(cholesky)/cholesky | solution.py:94
  524.3 0.1 cholesky.224
  524.4 9.8 %custom-call.27 = f32[1,128,128]{1,2,0:T(8,128)S(1)} custom-call(f32[1,128,128]{2,1,0:T(8,128)S(1)} %get-tuple-element.23), custom_call_target="InvertDiagBlocksLowerTriangular" | custom-call | tf_op jit(solution)/shard_map/jit(cholesky)/cholesky | solution.py:94
  534.2 0.3 constant_dynamic-update-slice_fusion.6
  534.5 0.3 convolution_subtract_fusion
  534.9 11.7 %cholesky.217 = f32[128,128]{1,0:T(8,128)S(1)} custom-call(f32[128,128]{1,0:T(8,128)S(1)} %cholesky.270), custom_call_target="Cholesky" | custom-call | tf_op jit(solution)/shard_map/jit(cholesky)/cholesky | solution.py:94
  546.6 10.0 %custom-call.28 = f32[1,128,128]{1,2,0:T(8,128)S(1)} custom-call(f32[1,128,128]{2,1,0:T(8,128)S(1)} %get-tuple-element.20), custom_call_target="InvertDiagBlocksLowerTriangular" | custom-call | tf_op jit(solution)/shard_map/jit(cholesky)/cholesky | solution.py:94
  556.6 0.3 convolution_dynamic-update-slice_fusion
  556.9 0.4 convolution_subtract_fusion.1
  557.3 11.7 %cholesky.238 = f32[128,128]{1,0:T(8,128)S(1)} custom-call(f32[128,128]{1,0:T(8,128)S(1)} %cholesky.275), custom_call_target="Cholesky" | custom-call | tf_op jit(solution)/shard_map/jit(cholesky)/cholesky | solution.py:94
  569.0 9.8 %custom-call.29 = f32[1,128,128]{1,2,0:T(8,128)S(1)} custom-call(f32[1,128,128]{2,1,0:T(8,128)S(1)} %get-tuple-element.17), custom_call_target="InvertDiagBlocksLowerTriangular" | custom-call | tf_op jit(solution)/shard_map/jit(cholesky)/cholesky | solution.py:94
  578.9 0.2 convolution_dynamic-update-slice_fusion.1
  579.1 0.4 convolution_subtract_fusion.2
  579.5 11.7 %cholesky.255 = f32[128,128]{1,0:T(8,128)S(1)} custom-call(f32[128,128]{1,0:T(8,128)S(1)} %convolution_subtract_fusion.2), custom_call_target="Cholesky" | custom-call | tf_op jit(solution)/shard_map/jit(cholesky)/cholesky | solution.py:94
  591.2 0.7 compare_reduce_fusion.1
  591.9 0.6 compare_reduce_fusion
  592.6 0.7 compare_reduce_fusion.2
  595.8 0.1 select_bitcast_fusion
  595.9 1.3 copy.21
  (18 shorter events, 0.4 us)
Async XLA Ops:
  7.9 15.2 %collective-permute-start = (f32[16,512]{1,0:T(8,128)S(1)}, f32[16,512]{1,0:T(8,128)S(1)}, u32[]{:S(2)}, u32[]{:S(2)}) collective-permute-start(f32[16,512]{1,0:T(8,128)S(1)} %get-tuple-element.12), channel_id=1, source_target_pairs={{0,1},{1,2},{2,3},{3,4},{4,5},{5,6},{6,7},{7,8},{8,9},{9,10},{10,1... | collective-permute-start | bytes 98312 | tf_op jit(solution)/shard_map/ppermute | solution.py:15
  12.3 23.0 %collective-permute-start.1 = (f32[16,512]{1,0:T(8,128)S(1)}, f32[16,512]{1,0:T(8,128)S(1)}, u32[]{:S(2)}, u32[]{:S(2)}) collective-permute-start(f32[16,512]{1,0:T(8,128)S(1)} %get-tuple-element.13), channel_id=1, source_target_pairs={{1,0},{2,1},{3,2},{4,3},{5,4},{6,5},{7,6},{8,7},{9,8},{10,9},{11,1... | collective-permute-start | bytes 98312 | tf_op jit(solution)/shard_map/ppermute | solution.py:16
  211.8 111.4 %all-to-all-start = ((f32[128,32,512]{2,1,0:T(8,128)}), f32[128,32,512]{2,1,0:T(8,128)}, u32[]{:S(2)}, u32[]{:S(2)}) async-start(f32[128,32,512]{2,1,0:T(8,128)} %broadcast_select_fusion), calls=%async_computation | async-start | bytes 16777216 | tf_op jit(solution)/shard_map/all_to_all | solution.py:74
  220.7 177.8 %all-reduce.4.cloned.1.call-start = ((), (), s32[]{:S(2)}) async-start(), calls=%async_computation.1 | async-start | bytes 2097152 | tf_op jit(solution)/shard_map/psum | solution.py:93
  353.1 242.8 %copy-start = (f32[64,512]{1,0:T(8,128)}, f32[64,512]{1,0:T(8,128)S(1)}, u32[]{:S(2)}) copy-start(f32[64,512]{1,0:T(8,128)S(1)} %broadcast_select_fusion.1) | copy-start | bytes 393220
  355.1 154.3 %all-reduce.6.cloned.1.call-start = ((), (), s32[]{:S(2)}) async-start(), calls=%async_computation.2 | async-start | bytes 2097152 | tf_op jit(solution)/shard_map/psum | solution.py:93
Sparse Core Ops, SparseCore 0:
  355.2 43.2 all-reduce.3
  401.7 107.6 all-reduce.5
